TPU v7x, 32 devices: a whole 2x2x4 slice. The times are simulated.
32 devices in a mesh: grp: 2 (over y), ia: 4 (over z), ja: 4 (over x, core).
Axes of the slice: x: 2, y: 2, z: 4, core: 2. Of those that a mesh axis runs over, the one named last changes fastest.
Arguments:
- doubles: bfloat16 [8, 16, 384, 384], P(('grp', 'ia'), 'ja'), parts along dimension 0, may hold values from -6 to 6
- aux_factors: bfloat16 [4, 384, 384], P('ia'), may hold values from -0.15625 to 0.15625
- cycle_factors: bfloat16 [16, 384, 128], replicated, may hold values from -0.21875 to 0.21875
Outputs:
- sigma: bfloat16 [8, 16, 384, 384], P(('grp', 'ia'), 'ja'), parts along dimension 0
There are 2 independent parts, one for each index of `grp`. A program takes and returns all parts, laid end to end along the dimension named above; an argument that names none is the same for every part. Nothing has to cross between parts.
All inputs are finite; a program needn't handle non-finite values.
Results may differ from a plain program's by a relative error of at most 0.008.
Values may be sent and summed in bfloat16 or wider, within the bound.
A program may use at most 128 MiB of HBM per device.

v0:
```python
import functools

import jax
import jax.numpy as jnp
from jax import lax
from jax.experimental import pallas as pl
from jax.experimental.pallas import tpu as pltpu
from jax.sharding import PartitionSpec as P

MESH = pl.DeviceIdType.MESH
F32 = jnp.float32
BF16 = jnp.bfloat16
NT = (((1,), (1,)), ((), ()))
CORES = 2


def sigma_kernel(n, nj, ny, d_hbm, aux_hbm, u_hbm, out, d, u, aux, half, acc,
                 plat, lat_in, lat, load_sem, z_send, z_recv, x_send, x_recv,
                 s_send, s_recv, p_send, p_recv, l_send, l_recv):
    nx = nj // CORES
    pairs_j, width = d.shape[0], d.shape[1]
    grp_j = half.shape[2] // width
    n_jp = pairs_j // grp_j
    rows = width // (ny * nj)
    lat_rows = width // nj
    iz = lax.axis_index("ia")
    iy = lax.axis_index("grp") if ny > 1 else 0
    ij = lax.axis_index("ja")
    sibling = ij ^ 1

    def chunk(owner):
        return pl.ds(pl.multiple_of(owner * rows, rows), rows)

    def lat_chunk(owner):
        return pl.ds(pl.multiple_of(owner * lat_rows, lat_rows), lat_rows)

    def piece(m, base):
        return chunk((iy ^ (m // nx)) * nj + (base ^ (CORES * (m % nx))))

    def slot(k):
        return pl.ds(k * width, width)

    load_aux = pltpu.make_async_copy(aux_hbm.at[0], aux.at[:, slot(0)], load_sem.at[0])
    load_d = pltpu.make_async_copy(d_hbm.at[0], d, load_sem.at[1])
    load_u = pltpu.make_async_copy(
        u_hbm.at[pl.ds(ij * pairs_j, pairs_j)], u, load_sem.at[2])
    load_aux.start()
    load_d.start()
    load_u.start()

    def plane(m):
        where = {"ja": ij ^ (CORES * (m % nx))}
        if m >= nx:
            where["grp"] = iy ^ (m // nx)
        return where

    barrier = pltpu.get_barrier_semaphore()
    for k in range(1, n):
        pl.semaphore_signal(barrier, inc=1, device_id={"ia": iz ^ k}, device_id_type=MESH)
    for m in range(1, nj):
        pl.semaphore_signal(barrier, inc=1, device_id={"ja": ij ^ m}, device_id_type=MESH)
    for m in range(nx, ny * nx):
        pl.semaphore_signal(barrier, inc=1, device_id=plane(m), device_id_type=MESH)
    pl.semaphore_wait(barrier, n - 1 + nj - 1 + (ny - 1) * nx)

    def remote(src, dst, send, recv, where):
        return pltpu.make_async_remote_copy(
            src_ref=src, dst_ref=dst, send_sem=send, recv_sem=recv,
            device_id=where, device_id_type=MESH)

    def z_copy(k):
        return remote(aux.at[piece(0, ij), slot(0)], aux.at[piece(0, ij), slot(k)],
                      z_send.at[k], z_recv.at[k], {"ia": iz ^ k})

    def x_copy(k, m, from_m=0):
        part = aux.at[piece(from_m, ij), slot(k)]
        return remote(part, part, x_send.at[k, m], x_recv.at[k, m], plane(m))

    def s_copy(k, m, base):
        part = aux.at[piece(m, base), slot(k)]
        return remote(part, part, s_send.at[k, m], s_recv.at[k, m], {"ja": sibling})

    def p_copy(m):
        return remote(plat.at[lat_chunk(ij ^ m)], lat_in.at[m], p_send.at[m], p_recv.at[m],
                      {"ja": ij ^ m})

    def l_copy(m, owner):
        return remote(lat.at[lat_chunk(owner)], lat.at[lat_chunk(owner)], l_send.at[m],
                      l_recv.at[m], {"ja": ij ^ m})

    load_aux.wait()
    for k in range(1, n):
        z_copy(k).start()

    load_d.wait()
    load_u.wait()

    total = jnp.zeros(plat.shape, F32)
    for j in range(pairs_j):
        total += jnp.dot(d[j], u[j], preferred_element_type=F32)
    plat[...] = total.astype(BF16)

    def halfway(k, place):
        factor = aux[:, k * width:(k + 1) * width]

        @pl.loop(0, n_jp)
        def _(jp):
            for t in range(grp_j):
                block = lax.dot_general(d[jp * grp_j + t], factor, NT,
                                        preferred_element_type=F32)
                half[jp, place * width:(place + 1) * width,
                     t * width:(t + 1) * width] = block.astype(BF16)

    halfway(0, 0)
    for m in range(1, nj):
        p_copy(m).start()

    passed, relayed = set(), set()

    def pass_on(k):
        if k >= n or k in passed:
            return
        passed.add(k)
        z_copy(k).wait_recv()
        for m in range(1, ny * nx):
            x_copy(k, m).start()
        s_copy(k, 0, ij).start()

    def relay(k):
        if k >= n or k in relayed:
            return
        relayed.add(k)
        for m in range(1, ny * nx):
            x_copy(k, m, m).wait_recv()
            s_copy(k, m, ij).start()

    def gather_latent():
        mine = plat[lat_chunk(ij), :].astype(F32)
        for m in range(1, nj):
            p_copy(m).wait_recv()
            mine += lat_in[m].astype(F32)
        lat[lat_chunk(ij), :] = mine.astype(BF16)

    def send_latent():
        for m in range(1, nj):
            l_copy(m, ij).start()

    def ladder(first, count, last):
        @pl.loop(0, n_jp)
        def _(jp):
            res = jnp.dot(aux[:, first * width:(first + count) * width],
                          half[jp, :count * width, :], preferred_element_type=F32)
            if first > 0:
                res += acc[jp]
            if not last:
                acc[jp] = res
            else:
                for t in range(grp_j):
                    j = jp * grp_j + t
                    cyc = lax.dot_general(lat[...], u[j], NT, preferred_element_type=F32)
                    out[0, j] = (res[:, t * width:(t + 1) * width] + cyc).astype(BF16)

    def latent_all():
        for m in range(1, nj):
            l_copy(m, ij ^ m).wait_recv()

    pass_on(1)
    pass_on(2)
    gather_latent()
    relay(1)
    pass_on(3)
    send_latent()
    if n == 1:
        latent_all()
        ladder(0, 1, True)
    for k in range(1, n):
        for m in range(ny * nx):
            s_copy(k, m, sibling).wait_recv()
        halfway(k, k % 2)
        relay(k + 1)
        pass_on(k + 3)
        if k == n - 1:
            latent_all()
        if k % 2 == 1:
            relay(k + 2)
            ladder(k - 1, 2, k == n - 1)
        elif k == n - 1:
            ladder(k, 1, True)

    for k in range(1, n):
        z_copy(k).wait_send()
        for m in range(1, ny * nx):
            x_copy(k, m).wait_send()
        for m in range(ny * nx):
            s_copy(k, m, ij).wait_send()
    for m in range(1, nj):
        p_copy(m).wait_send()
        l_copy(m, ij).wait_send()


def shards(n, nj, grps, doubles, aux_factors, cycle_factors):
    _, pairs_j, width, _ = doubles.shape
    rank = cycle_factors.shape[2]
    grp_j = 2 if pairs_j % 2 == 0 else 1
    ny = grps if width % (grps * nj * 16) == 0 else 1
    nx = nj // CORES * ny
    dma = pltpu.SemaphoreType.DMA
    hbm = pl.BlockSpec(memory_space=pltpu.HBM)
    flops = 4 * n * pairs_j * width**3 + 4 * pairs_j * width * width * rank
    return pl.pallas_call(
        functools.partial(sigma_kernel, n, nj, ny),
        out_shape=pltpu.VMEM(doubles.shape, BF16),
        in_specs=[hbm] * 3,
        out_specs=pl.BlockSpec(memory_space=pltpu.VMEM),
        scratch_shapes=[
            pltpu.VMEM((pairs_j, width, width), BF16),
            pltpu.VMEM((pairs_j, width, rank), BF16),
            pltpu.VMEM((width, n * width), BF16),
            pltpu.VMEM((pairs_j // grp_j, 2 * width, grp_j * width), BF16),
            pltpu.VMEM((pairs_j // grp_j, width, grp_j * width), F32),
            pltpu.VMEM((width, rank), BF16),
            pltpu.VMEM((nj, width // nj, rank), BF16),
            pltpu.VMEM((width, rank), BF16),
            dma((3,)),
            dma((n,)), dma((n,)),
            dma((n, nx)), dma((n, nx)),
            dma((n, nx)), dma((n, nx)),
            dma((nj,)), dma((nj,)),
            dma((nj,)), dma((nj,)),
        ],
        compiler_params=pltpu.CompilerParams(
            collective_id=0, has_side_effects=True, vmem_limit_bytes=67043328 - doubles.size * 2 - 2**16),
        cost_estimate=pl.CostEstimate(
            flops=flops, bytes_accessed=4 * doubles.size, transcendentals=0),
    )(doubles, aux_factors, cycle_factors)


def solution(mesh):
    in_specs = (P(("grp", "ia"), "ja", None, None), P("ia", None, None), P())
    out_specs = P(("grp", "ia"), "ja", None, None)
    body = functools.partial(shards, mesh.shape["ia"], mesh.shape["ja"], mesh.shape["grp"])
    return jax.shard_map(body, mesh=mesh, in_specs=in_specs, out_specs=out_specs, check_vma=False)
```

profile of v0, /device:TPU:0, one launch (start us, length us, event | category | flops | bytes accessed | tf_op | source)
XLA Modules:
  0.0 22.9 jit_solution(14534339885267477921)
XLA Ops:
  0.0 21.8 %shard_map.37 = bf16[1,4,384,384]{3,2,1,0:T(8,128)(2,1)S(1)} custom-call(bf16[1,4,384,384]{3,2,1,0:T(8,128)(2,1)} %d_hbm.1, bf16[1,384,384]{2,1,0:T(8,128)(2,1)} %aux_hbm.1, bf16[16,384,128]{2,1,0:T(8,128)(2,1)} %u_hbm.1), custom_call_target="tpu_custom_call" | custom-call | flops 3925868544 | bytes 2359296 | tf_op jit(solution)/shard_map/pallas_call | solution.py:210
  21.8 1.0 %copy.5 = bf16[1,4,384,384]{3,2,1,0:T(8,128)(2,1)} copy(bf16[1,4,384,384]{3,2,1,0:T(8,128)(2,1)S(1)} %shard_map.37) | data formatting | bytes 2359296
where the time goes:
time: 23 us; the launch traced here: 22.9 us
  Pallas kernels  21.8 us (95%)
  local copies, waits for them, and re-layouts  1.02 us (4%)
    pallas_call x1, Pallas kernels, shards(): pl.pallas_call(functools.partial(sigma_kernel, n, nj, ny), out_shape=pltp...  21.8 us
    unnamed x1, local copies, waits for them, and re-layouts  1.02 us

commit v1 on v0

v1 whole, which is shorter than its diff:
```python
import functools

import jax
import jax.numpy as jnp
from jax import lax
from jax.experimental import pallas as pl
from jax.experimental.pallas import tpu as pltpu
from jax.sharding import PartitionSpec as P

MESH = pl.DeviceIdType.MESH
F32 = jnp.float32
BF16 = jnp.bfloat16
NT = (((1,), (1,)), ((), ()))
CORES = 2
LAST_STAGE = 4


def sigma_kernel(n, nj, ny, d_hbm, aux_hbm, u_hbm, out, d, u, aux, half, acc,
                 plat, lat_own, lat_sib, lat_in, lat, load_sem, d_sem,
                 z_ready, x_ready, y_ready, s_ready, z_send, z_recv, r_send, r_recv,
                 s_send, s_recv, p_send, p_recv, l_send, l_recv):
    nx = nj // CORES
    pairs_j, width, _ = d.shape
    rows = width // (ny * nj)
    lat_rows = width // CORES
    iz = lax.axis_index("ia")
    iy = lax.axis_index("grp") if ny > 1 else 0
    ij = lax.axis_index("ja")
    core = ij % CORES
    sibling = {"ja": ij ^ 1}
    spots = [(y, x) for y in range(ny) for x in range(nx)]
    direct = [0] + [m for m, (y, x) in enumerate(spots) if y > 0 and x > 0]
    relayed = [m for m in range(1, len(spots)) if m not in direct]

    def piece(m, base):
        y, x = spots[m]
        owner = (iy ^ y) * nj + (base ^ (CORES * x))
        return pl.ds(pl.multiple_of(owner * rows, rows), rows)

    def lat_half(c):
        return pl.ds(pl.multiple_of(c * lat_rows, lat_rows), lat_rows)

    def plane(m):
        y, x = spots[m]
        return {"grp": iy ^ y} if x == 0 else {"ja": ij ^ (CORES * x)}

    load_aux = pltpu.make_async_copy(aux_hbm.at[0], aux.at[0], load_sem.at[0])
    load_u = pltpu.make_async_copy(
        u_hbm.at[pl.ds(ij * pairs_j, pairs_j)], u, load_sem.at[1])

    def load_d(j):
        return pltpu.make_async_copy(d_hbm.at[0, j], d.at[j], d_sem.at[j])

    load_u.start()
    for j in range(pairs_j):
        load_d(j).start()
    load_aux.start()

    def remote(src, dst, send, recv, where):
        return pltpu.make_async_remote_copy(
            src_ref=src, dst_ref=dst, send_sem=send, recv_sem=recv,
            device_id=where, device_id_type=MESH)

    def z_copy(k, m, src=aux.at[0]):
        return remote(src.at[piece(m, ij)], aux.at[k, piece(m, ij)],
                      z_send.at[k - 1], z_recv.at[(k - 1) * len(direct) + direct.index(m)],
                      {"ia": iz ^ k})

    def r_copy(k, m, from_m=0):
        part = aux.at[k, piece(from_m, ij)]
        return remote(part, part, r_send.at[k - 1],
                      r_recv.at[(k - 1) * len(relayed) + relayed.index(m)], plane(m))

    def s_copy(k, m, base):
        part = aux.at[k, piece(m, base)]
        return remote(part, part, s_send.at[k - 1], s_recv.at[k - 1], sibling)

    def sent(k, count, sem):
        part = aux.at[k, pl.ds(0, count * rows)]
        return pltpu.make_async_copy(part, part, sem.at[k - 1])

    def p_copy(x):
        if x == 0:
            return remote(plat, lat_sib, p_send.at[0], p_recv.at[0], sibling)
        return remote(plat.at[lat_half(core)], lat_in.at[x], p_send.at[x], p_recv.at[x],
                      {"ja": ij ^ (CORES * x)})

    def l_copy(c):
        return remote(lat.at[lat_half(c)], lat.at[lat_half(c)], l_send, l_recv, sibling)

    def signal(sem, where):
        pl.semaphore_signal(sem, inc=1, device_id=where, device_id_type=MESH)

    partners = [(iz ^ k, iz, {"ia": iz ^ k}, z_ready.at[k]) for k in range(1, n)]
    partners += [(ij ^ (CORES * x), ij, {"ja": ij ^ (CORES * x)}, x_ready.at[x])
                 for x in range(1, nx)]
    partners += [(ij ^ 1, ij, sibling, s_ready)]
    partners += [(iy ^ y, iy, {"grp": iy ^ y}, y_ready.at[y]) for y in range(1, ny)]

    barrier = pltpu.get_barrier_semaphore()
    for other, me, where, _ in partners:
        @pl.when(other > me)
        def _():
            signal(barrier, where)
    lower = iz + ij // CORES + core + iy

    @pl.when(lower > 0)
    def _():
        pl.semaphore_wait(barrier, lower)

    def await_ready(index):
        other, me, _, ready = partners[index]

        @pl.when(other > me)
        def _():
            pl.semaphore_wait(ready, 1)

    def send_down(stage):
        for t in range(n - 1):
            for near in (True, False):
                turns = [m for m in direct
                         if min(min(t + 1, 2) if near else t + 1 + (m > 0), LAST_STAGE) == stage]
                if turns:
                    @pl.when(t == iz - 1 if near else t < iz - 1)
                    def _():
                        for m in turns:
                            z_copy(iz ^ t, m, aux_hbm.at[0] if stage == 1 else aux.at[0]).start()

    def send_up(first, near, who):
        for t in range(1, n):
            turns = direct[:1] if first else direct[1:]
            if first and near:
                turns = direct
            @pl.when((t == iz + 1 if near else t > iz + 1) & who)
            def _():
                if first:
                    pl.semaphore_wait(z_ready.at[iz ^ t], 1)
                for m in turns:
                    z_copy(iz ^ t, m).start()

    send_down(1)
    for other, me, where, ready in partners:
        @pl.when(other < me)
        def _():
            signal(ready, where)

    with jax.named_scope("latent"):
        load_u.wait()
        total = jnp.zeros(lat_own.shape, F32)
        for j in range(pairs_j):
            load_d(j).wait()
            total += jnp.dot(d[j], u[j], preferred_element_type=F32)
        lat_own[...] = total
        plat[...] = total.astype(BF16)

    load_aux.wait()
    send_down(2)
    send_up(True, True, iz > 0)

    def halfway(k, place):
        for j in range(pairs_j):
            block = lax.dot_general(d[j], aux[k], NT, preferred_element_type=F32)
            half[place * width:(place + 1) * width,
                 j * width:(j + 1) * width] = block.astype(BF16)

    def ladder(k):
        return jnp.dot(aux[k], half[:width, :], preferred_element_type=F32)

    def finish(ks):
        left = jnp.concatenate([aux[k] for k in ks] + [lat[...]], axis=1)
        res = jnp.dot(left, half[(2 - len(ks)) * width:, :], preferred_element_type=F32)
        if n > 1:
            res += acc[...]
        for j in range(pairs_j):
            out[0, j] = res[:, j * width:(j + 1) * width].astype(BF16)

    for j in range(pairs_j):
        half[2 * width:, j * width:(j + 1) * width] = u[j].T

    with jax.named_scope("own"):
        halfway(0, 0 if n > 1 else 1)
    send_down(3)
    send_up(True, True, iz == 0)
    send_up(True, False, iz > 0)
    for index in range(n - 1, len(partners)):
        await_ready(index)
    p_copy(0).start()
    with jax.named_scope("ownlad"):
        if n > 1:
            acc[...] = ladder(0)
    send_down(4)
    with jax.named_scope("up"):
        send_up(True, False, iz == 0)

    def pass_on(k):
        with jax.named_scope("pass%d" % k):
            z_copy(k, 0).wait_recv()
            for m in relayed:
                r_copy(k, m).start()
            s_copy(k, 0, ij).start()

    def share(k):
        with jax.named_scope("shareA%d" % k):
            for m in direct[1:]:
                z_copy(k, m).wait_recv()
                s_copy(k, m, ij).start()
        with jax.named_scope("shareB%d" % k):
            for m in relayed:
                r_copy(k, m, m).wait_recv()
                s_copy(k, m, ij).start()

    def complete(k):
        with jax.named_scope("compl%d" % k):
            sent(k, len(spots), s_recv).wait()

    def chip_latent():
        p_copy(0).wait_recv()
        lat_own[...] += lat_sib[...].astype(F32)
        p_copy(0).wait_send()
        plat[...] = lat_own[...].astype(BF16)

    def cross_latent():
        for x in range(1, nx):
            p_copy(x).start()

    def whole_latent():
        with jax.named_scope("wholelat"):
            mine = lat_own[lat_half(core), :]
            for x in range(1, nx):
                p_copy(x).wait_recv()
                mine += lat_in[x].astype(F32)
            lat[lat_half(core), :] = mine.astype(BF16)

    chip_latent()
    if n > 1:
        pass_on(1)
    send_up(False, False, iz >= 0)
    for k in range(2, min(4, n)):
        pass_on(k)
    cross_latent()
    for k in range(1, min(2, n)):
        share(k)
    last = list(range(max(n - 2, min(n - 1, 1)), n))
    for k in range(1, last[0]):
        complete(k)
        with jax.named_scope("half%d" % k):
            halfway(k, 0)
        share(k + 1)
        if k + 3 < n:
            pass_on(k + 3)
        with jax.named_scope("lad%d" % k):
            acc[...] += ladder(k)
    whole_latent()
    l_copy(core).start()
    for place, k in enumerate(last):
        if place == 0 and len(last) > 1:
            share(last[1])
        if k > 0:
            complete(k)
            with jax.named_scope("half%d" % k):
                halfway(k, 2 - len(last) + place)
    l_copy(core ^ 1).wait_recv()
    with jax.named_scope("final"):
        finish(last)

    with jax.named_scope("tail"):
        for k in range(1, n):
            sent(k, len(direct), z_send).wait()
            if relayed:
                sent(k, len(relayed), r_send).wait()
            sent(k, len(spots), s_send).wait()
        for x in range(1, nx):
            p_copy(x).wait_send()
        l_copy(core).wait_send()


def shards(n, nj, grps, doubles, aux_factors, cycle_factors):
    _, pairs_j, width, _ = doubles.shape
    rank = cycle_factors.shape[2]
    nx = nj // CORES
    ny = grps if width % (grps * nj * 16) == 0 else 1
    others = max(n - 1, 1)
    ahead = 1 + (nx - 1) * (ny - 1)
    dma = pltpu.SemaphoreType.DMA
    flag = pltpu.SemaphoreType.REGULAR
    hbm = pl.BlockSpec(memory_space=pltpu.HBM)
    flops = 4 * n * pairs_j * width**3 + 4 * pairs_j * width * width * rank
    return pl.pallas_call(
        functools.partial(sigma_kernel, n, nj, ny),
        out_shape=pltpu.VMEM(doubles.shape, BF16),
        in_specs=[hbm] * 3,
        out_specs=pl.BlockSpec(memory_space=pltpu.VMEM),
        scratch_shapes=[
            pltpu.VMEM((pairs_j, width, width), BF16),
            pltpu.VMEM((pairs_j, width, rank), BF16),
            pltpu.VMEM((n, width, width), BF16),
            pltpu.VMEM((2 * width + rank, pairs_j * width), BF16),
            pltpu.VMEM((width, pairs_j * width), F32),
            pltpu.VMEM((width, rank), BF16),
            pltpu.VMEM((width, rank), F32),
            pltpu.VMEM((width, rank), BF16),
            pltpu.VMEM((nx, width // CORES, rank), BF16),
            pltpu.VMEM((width, rank), BF16),
            dma((2,)), dma((pairs_j,)),
            flag((n,)), flag((nx,)), flag((ny,)), flag,
            dma((others,)), dma((others * ahead,)),
            dma((others,)), dma((others * max(nx * ny - ahead, 1),)),
            dma((others,)), dma((others,)),
            dma((nx,)), dma((nx,)),
            dma, dma,
        ],
        compiler_params=pltpu.CompilerParams(
            collective_id=0, has_side_effects=True, vmem_limit_bytes=67043328 - doubles.size * 2 - 2**16),
        cost_estimate=pl.CostEstimate(
            flops=flops, bytes_accessed=4 * doubles.size, transcendentals=0),
    )(doubles, aux_factors, cycle_factors)


def solution(mesh):
    in_specs = (P(("grp", "ia"), "ja", None, None), P("ia", None, None), P())
    out_specs = P(("grp", "ia"), "ja", None, None)
    body = functools.partial(shards, mesh.shape["ia"], mesh.shape["ja"], mesh.shape["grp"])
    return jax.shard_map(body, mesh=mesh, in_specs=in_specs, out_specs=out_specs, check_vma=False)
```

time: 23 us -> 19 us (0.83)
  the two profiles are of different devices: /device:TPU:0 before, /device:TPU:17 now
where the time goes in v1:
time: 19 us; the launch traced here: 18.8 us
  Pallas kernels  17.8 us (94%)
  local copies, waits for them, and re-layouts  1.02 us (5%)
    pallas_call x1, Pallas kernels, shards(): pl.pallas_call(functools.partial(sigma_kernel, n, nj, ny), out_shape=pltp...  17.8 us
    unnamed x1, local copies, waits for them, and re-layouts  1.02 us

profile of v1, /device:TPU:17, one launch (start us, length us, event | category | flops | bytes accessed | tf_op | source)
XLA Modules:
  0.0 18.8 jit_solution(2766519663240863752)
XLA Ops:
  0.0 17.8 %shard_map.37 = bf16[1,4,384,384]{3,2,1,0:T(8,128)(2,1)S(1)} custom-call(bf16[1,4,384,384]{3,2,1,0:T(8,128)(2,1)} %d_hbm.1, bf16[1,384,384]{2,1,0:T(8,128)(2,1)} %aux_hbm.1, bf16[16,384,128]{2,1,0:T(8,128)(2,1)} %u_hbm.1), custom_call_target="tpu_custom_call" | custom-call | flops 3925868544 | bytes 2359296 | tf_op jit(solution)/shard_map/pallas_call | solution.py:288
  17.8 1.0 %copy.5 = bf16[1,4,384,384]{3,2,1,0:T(8,128)(2,1)} copy(bf16[1,4,384,384]{3,2,1,0:T(8,128)(2,1)S(1)} %shard_map.37) | data formatting | bytes 2359296

commit v2 on v1

--- a/solution.py
+++ b/solution.py
@@ -12,7 +12,8 @@
 BF16 = jnp.bfloat16
 NT = (((1,), (1,)), ((), ()))
 CORES = 2
-LAST_STAGE = 4
+LAST_STAGE = 5
+SPLIT = 1
 
 
 def sigma_kernel(n, nj, ny, d_hbm, aux_hbm, u_hbm, out, d, u, aux, half, acc,
@@ -48,12 +49,19 @@
     load_u = pltpu.make_async_copy(
         u_hbm.at[pl.ds(ij * pairs_j, pairs_j)], u, load_sem.at[1])
 
-    def load_d(j):
-        return pltpu.make_async_copy(d_hbm.at[0, j], d.at[j], d_sem.at[j])
+    def load_d(j, part):
+        share_of = pl.ds(part * (width // SPLIT), width // SPLIT)
+        return pltpu.make_async_copy(d_hbm.at[0, j, share_of], d.at[j, share_of],
+                                     d_sem.at[j])
+
+    orders = [sorted(range(1, n), key=lambda k: (abs((z ^ k) - z) if z ^ k < z else n, k)) for z in range(n)]
+    order = [0] + [sum(jnp.where(iz == z, orders[z][i], 0) for z in range(n))
+                   for i in range(n - 1)]
 
     load_u.start()
     for j in range(pairs_j):
-        load_d(j).start()
+        for part in range(SPLIT):
+            load_d(j, part).start()
     load_aux.start()
 
     def remote(src, dst, send, recv, where):
@@ -115,16 +123,21 @@
         def _():
             pl.semaphore_wait(ready, 1)
 
+    def stage_of(t, m, near):
+        if t == 0:
+            return 1 + (m > 0) * (0 if near else 2)
+        return 3 if near else t + 2 + (m > 0)
+
     def send_down(stage):
         for t in range(n - 1):
             for near in (True, False):
                 turns = [m for m in direct
-                         if min(min(t + 1, 2) if near else t + 1 + (m > 0), LAST_STAGE) == stage]
+                         if min(stage_of(t, m, near), LAST_STAGE) == stage]
                 if turns:
                     @pl.when(t == iz - 1 if near else t < iz - 1)
                     def _():
                         for m in turns:
-                            z_copy(iz ^ t, m, aux_hbm.at[0] if stage == 1 else aux.at[0]).start()
+                            z_copy(iz ^ t, m, aux_hbm.at[0] if stage < 3 else aux.at[0]).start()
 
     def send_up(first, near, who):
         for t in range(1, n):
@@ -148,23 +161,30 @@
         load_u.wait()
         total = jnp.zeros(lat_own.shape, F32)
         for j in range(pairs_j):
-            load_d(j).wait()
+            pltpu.make_async_copy(d_hbm.at[0, j], d.at[j], d_sem.at[j]).wait()
+            if j == 0:
+                send_down(2)
             total += jnp.dot(d[j], u[j], preferred_element_type=F32)
         lat_own[...] = total
         plat[...] = total.astype(BF16)
 
     load_aux.wait()
-    send_down(2)
+    send_down(3)
     send_up(True, True, iz > 0)
 
-    def halfway(k, place):
-        for j in range(pairs_j):
+    def halfway(k, place, pairs):
+        for j in pairs:
             block = lax.dot_general(d[j], aux[k], NT, preferred_element_type=F32)
             half[place * width:(place + 1) * width,
                  j * width:(j + 1) * width] = block.astype(BF16)
 
-    def ladder(k):
-        return jnp.dot(aux[k], half[:width, :], preferred_element_type=F32)
+    def ladder(k, pairs, add):
+        cols = slice(pairs[0] * width, (pairs[-1] + 1) * width)
+        res = jnp.dot(aux[k], half[:width, cols], preferred_element_type=F32)
+        acc[:, cols] = acc[:, cols] + res if add else res
+
+    every = list(range(pairs_j))
+    early, late = every[:(pairs_j + 1) // 2], every[(pairs_j + 1) // 2:] or every[-1:]
 
     def finish(ks):
         left = jnp.concatenate([aux[k] for k in ks] + [lat[...]], axis=1)
@@ -178,8 +198,8 @@
         half[2 * width:, j * width:(j + 1) * width] = u[j].T
 
     with jax.named_scope("own"):
-        halfway(0, 0 if n > 1 else 1)
-    send_down(3)
+        halfway(0, 0 if n > 1 else 1, every)
+    send_down(4)
     send_up(True, True, iz == 0)
     send_up(True, False, iz > 0)
     for index in range(n - 1, len(partners)):
@@ -187,30 +207,33 @@
     p_copy(0).start()
     with jax.named_scope("ownlad"):
         if n > 1:
-            acc[...] = ladder(0)
-    send_down(4)
+            ladder(0, every, False)
+    send_down(5)
     with jax.named_scope("up"):
         send_up(True, False, iz == 0)
 
-    def pass_on(k):
-        with jax.named_scope("pass%d" % k):
+    def pass_on(i):
+        k = order[i]
+        with jax.named_scope("pass%d" % i):
             z_copy(k, 0).wait_recv()
             for m in relayed:
                 r_copy(k, m).start()
             s_copy(k, 0, ij).start()
 
-    def share(k):
-        with jax.named_scope("shareA%d" % k):
+    def share(i):
+        k = order[i]
+        with jax.named_scope("shareA%d" % i):
             for m in direct[1:]:
                 z_copy(k, m).wait_recv()
                 s_copy(k, m, ij).start()
-        with jax.named_scope("shareB%d" % k):
+        with jax.named_scope("shareB%d" % i):
             for m in relayed:
                 r_copy(k, m, m).wait_recv()
                 s_copy(k, m, ij).start()
 
-    def complete(k):
-        with jax.named_scope("compl%d" % k):
+    def complete(i):
+        k = order[i]
+        with jax.named_scope("compl%d" % i):
             sent(k, len(spots), s_recv).wait()
 
     def chip_latent():
@@ -232,36 +255,42 @@
             lat[lat_half(core), :] = mine.astype(BF16)
 
     chip_latent()
-    if n > 1:
-        pass_on(1)
+    for i in range(1, min(2, n)):
+        pass_on(i)
     send_up(False, False, iz >= 0)
-    for k in range(2, min(4, n)):
-        pass_on(k)
+    for i in range(2, min(4, n)):
+        pass_on(i)
     cross_latent()
-    for k in range(1, min(2, n)):
-        share(k)
+    for i in range(1, min(2, n)):
+        share(i)
     last = list(range(max(n - 2, min(n - 1, 1)), n))
-    for k in range(1, last[0]):
-        complete(k)
-        with jax.named_scope("half%d" % k):
-            halfway(k, 0)
-        share(k + 1)
-        if k + 3 < n:
-            pass_on(k + 3)
-        with jax.named_scope("lad%d" % k):
-            acc[...] += ladder(k)
+    for i in range(1, last[0]):
+        complete(i)
+        with jax.named_scope("halfA%d" % i):
+            halfway(order[i], 0, early)
+        share(i + 1)
+        with jax.named_scope("halfB%d" % i):
+            halfway(order[i], 0, late)
+        if i + 3 < n:
+            pass_on(i + 3)
+        with jax.named_scope("ladA%d" % i):
+            ladder(order[i], early, True)
+        if i == last[0] - 1 and len(last) > 1:
+            share(last[1])
+        with jax.named_scope("ladB%d" % i):
+            ladder(order[i], late, True)
     whole_latent()
     l_copy(core).start()
-    for place, k in enumerate(last):
-        if place == 0 and len(last) > 1:
-            share(last[1])
-        if k > 0:
-            complete(k)
-            with jax.named_scope("half%d" % k):
-                halfway(k, 2 - len(last) + place)
+    if last[0] == 1 and len(last) > 1:
+        share(last[1])
+    for place, i in enumerate(last):
+        if i > 0:
+            complete(i)
+            with jax.named_scope("half%d" % i):
+                halfway(order[i], 2 - len(last) + place, every)
     l_copy(core ^ 1).wait_recv()
     with jax.named_scope("final"):
-        finish(last)
+        finish([order[i] for i in last])
 
     with jax.named_scope("tail"):
         for k in range(1, n):

time: 19 us -> 19 us (level)
  the two profiles are of different devices: /device:TPU:17 before, /device:TPU:26 now
where the time goes in v2:
time: 19 us; the launch traced here: 18.8 us
  Pallas kernels  17.8 us (94%)
  local copies, waits for them, and re-layouts  1.02 us (5%)
    pallas_call x1, Pallas kernels, shards(): pl.pallas_call(functools.partial(sigma_kernel, n, nj, ny), out_shape=pltp...  17.8 us
    unnamed x1, local copies, waits for them, and re-layouts  1.02 us

profile of v2, /device:TPU:26, one launch (start us, length us, event | category | flops | bytes accessed | tf_op | source)
XLA Modules:
  0.0 18.8 jit_solution(17162957377360378997)
XLA Ops:
  0.0 17.8 %shard_map.37 = bf16[1,4,384,384]{3,2,1,0:T(8,128)(2,1)S(1)} custom-call(bf16[1,4,384,384]{3,2,1,0:T(8,128)(2,1)} %d_hbm.1, bf16[1,384,384]{2,1,0:T(8,128)(2,1)} %aux_hbm.1, bf16[16,384,128]{2,1,0:T(8,128)(2,1)} %u_hbm.1), custom_call_target="tpu_custom_call" | custom-call | flops 3925868544 | bytes 2359296 | tf_op jit(solution)/shard_map/pallas_call | solution.py:317
  17.8 1.0 %copy.5 = bf16[1,4,384,384]{3,2,1,0:T(8,128)(2,1)} copy(bf16[1,4,384,384]{3,2,1,0:T(8,128)(2,1)S(1)} %shard_map.37) | data formatting | bytes 2359296

commit v3 on v2

--- a/solution.py
+++ b/solution.py
@@ -197,7 +197,8 @@
     for j in range(pairs_j):
         half[2 * width:, j * width:(j + 1) * width] = u[j].T
 
-    with jax.named_scope("own"):
+    @pl.when(iz >= 0)
+    def _():
         halfway(0, 0 if n > 1 else 1, every)
     send_down(4)
     send_up(True, True, iz == 0)
@@ -205,7 +206,8 @@
     for index in range(n - 1, len(partners)):
         await_ready(index)
     p_copy(0).start()
-    with jax.named_scope("ownlad"):
+    @pl.when(iz >= 0)
+    def _():
         if n > 1:
             ladder(0, every, False)
     send_down(5)
@@ -266,18 +268,22 @@
     last = list(range(max(n - 2, min(n - 1, 1)), n))
     for i in range(1, last[0]):
         complete(i)
-        with jax.named_scope("halfA%d" % i):
+        @pl.when(iz >= 0)
+        def _():
             halfway(order[i], 0, early)
         share(i + 1)
-        with jax.named_scope("halfB%d" % i):
+        @pl.when(iz >= 0)
+        def _():
             halfway(order[i], 0, late)
         if i + 3 < n:
             pass_on(i + 3)
-        with jax.named_scope("ladA%d" % i):
+        @pl.when(iz >= 0)
+        def _():
             ladder(order[i], early, True)
         if i == last[0] - 1 and len(last) > 1:
             share(last[1])
-        with jax.named_scope("ladB%d" % i):
+        @pl.when(iz >= 0)
+        def _():
             ladder(order[i], late, True)
     whole_latent()
     l_copy(core).start()
@@ -286,10 +292,12 @@
     for place, i in enumerate(last):
         if i > 0:
             complete(i)
-            with jax.named_scope("half%d" % i):
+            @pl.when(iz >= 0)
+            def _():
                 halfway(order[i], 2 - len(last) + place, every)
     l_copy(core ^ 1).wait_recv()
-    with jax.named_scope("final"):
+    @pl.when(iz >= 0)
+    def _():
         finish([order[i] for i in last])
 
     with jax.named_scope("tail"):

time: 19 us -> 17.9 us (0.942)
  the two profiles are of different devices: /device:TPU:26 before, /device:TPU:27 now
where the time goes in v3:
time: 17.9 us; the launch traced here: 17.8 us
  Pallas kernels  16.8 us (94%)
  local copies, waits for them, and re-layouts  1.02 us (6%)
    pallas_call x1, Pallas kernels, shards(): pl.pallas_call(functools.partial(sigma_kernel, n, nj, ny), out_shape=pltp...  16.8 us
    unnamed x1, local copies, waits for them, and re-layouts  1.02 us

profile of v3, /device:TPU:27, one launch (start us, length us, event | category | flops | bytes accessed | tf_op | source)
XLA Modules:
  0.0 17.8 jit_solution(3158484112160857462)
XLA Ops:
  0.0 16.8 %shard_map.37 = bf16[1,4,384,384]{3,2,1,0:T(8,128)(2,1)S(1)} custom-call(bf16[1,4,384,384]{3,2,1,0:T(8,128)(2,1)} %d_hbm.1, bf16[1,384,384]{2,1,0:T(8,128)(2,1)} %aux_hbm.1, bf16[16,384,128]{2,1,0:T(8,128)(2,1)} %u_hbm.1), custom_call_target="tpu_custom_call" | custom-call | flops 3925868544 | bytes 2359296 | tf_op jit(solution)/shard_map/pallas_call | solution.py:325
  16.8 1.0 %copy.5 = bf16[1,4,384,384]{3,2,1,0:T(8,128)(2,1)} copy(bf16[1,4,384,384]{3,2,1,0:T(8,128)(2,1)S(1)} %shard_map.37) | data formatting | bytes 2359296

commit v4 on v3

--- a/solution.py
+++ b/solution.py
@@ -13,13 +13,14 @@
 NT = (((1,), (1,)), ((), ()))
 CORES = 2
 LAST_STAGE = 5
+NEAR_SECOND, FAR_SECOND, MID_FIRST, MID_SECOND, LAG = 3, 3, 2, 3, 1
 SPLIT = 1
 
 
 def sigma_kernel(n, nj, ny, d_hbm, aux_hbm, u_hbm, out, d, u, aux, half, acc,
                  plat, lat_own, lat_sib, lat_in, lat, load_sem, d_sem,
-                 z_ready, x_ready, y_ready, s_ready, z_send, z_recv, r_send, r_recv,
-                 s_send, s_recv, p_send, p_recv, l_send, l_recv):
+                 z_ready, x_ready, y_ready, s_ready, sends, prime_recv, late_recv, s_recv,
+                 p_send, p_recv, l_send, l_recv):
     nx = nj // CORES
     pairs_j, width, _ = d.shape
     rows = width // (ny * nj)
@@ -71,17 +72,16 @@
 
     def z_copy(k, m, src=aux.at[0]):
         return remote(src.at[piece(m, ij)], aux.at[k, piece(m, ij)],
-                      z_send.at[k - 1], z_recv.at[(k - 1) * len(direct) + direct.index(m)],
+                      sends.at[k - 1], (late_recv if m > 0 else prime_recv).at[k - 1],
                       {"ia": iz ^ k})
 
     def r_copy(k, m, from_m=0):
         part = aux.at[k, piece(from_m, ij)]
-        return remote(part, part, r_send.at[k - 1],
-                      r_recv.at[(k - 1) * len(relayed) + relayed.index(m)], plane(m))
+        return remote(part, part, sends.at[k - 1], late_recv.at[k - 1], plane(m))
 
     def s_copy(k, m, base):
         part = aux.at[k, piece(m, base)]
-        return remote(part, part, s_send.at[k - 1], s_recv.at[k - 1], sibling)
+        return remote(part, part, sends.at[k - 1], s_recv.at[k - 1], sibling)
 
     def sent(k, count, sem):
         part = aux.at[k, pl.ds(0, count * rows)]
@@ -99,11 +99,11 @@
     def signal(sem, where):
         pl.semaphore_signal(sem, inc=1, device_id=where, device_id_type=MESH)
 
-    partners = [(iz ^ k, iz, {"ia": iz ^ k}, z_ready.at[k]) for k in range(1, n)]
-    partners += [(ij ^ (CORES * x), ij, {"ja": ij ^ (CORES * x)}, x_ready.at[x])
+    partners = [(iz ^ k, iz, {"ia": iz ^ k}, z_ready.at[k - 1]) for k in range(1, n)]
+    partners += [(ij ^ (CORES * x), ij, {"ja": ij ^ (CORES * x)}, x_ready.at[x - 1])
                  for x in range(1, nx)]
     partners += [(ij ^ 1, ij, sibling, s_ready)]
-    partners += [(iy ^ y, iy, {"grp": iy ^ y}, y_ready.at[y]) for y in range(1, ny)]
+    partners += [(iy ^ y, iy, {"grp": iy ^ y}, y_ready.at[y - 1]) for y in range(1, ny)]
 
     barrier = pltpu.get_barrier_semaphore()
     for other, me, where, _ in partners:
@@ -125,8 +125,10 @@
 
     def stage_of(t, m, near):
         if t == 0:
-            return 1 + (m > 0) * (0 if near else 2)
-        return 3 if near else t + 2 + (m > 0)
+            return (NEAR_SECOND if near else FAR_SECOND) if m > 0 else 1
+        if near:
+            return MID_SECOND if m > 0 else MID_FIRST
+        return t + 2 + LAG * (m > 0)
 
     def send_down(stage):
         for t in range(n - 1):
@@ -147,7 +149,7 @@
             @pl.when((t == iz + 1 if near else t > iz + 1) & who)
             def _():
                 if first:
-                    pl.semaphore_wait(z_ready.at[iz ^ t], 1)
+                    pl.semaphore_wait(z_ready.at[(iz ^ t) - 1], 1)
                 for m in turns:
                     z_copy(iz ^ t, m).start()
 
@@ -194,6 +196,14 @@
         for j in range(pairs_j):
             out[0, j] = res[:, j * width:(j + 1) * width].astype(BF16)
 
+    def pass_on(i):
+        k = order[i]
+        with jax.named_scope("pass%d" % i):
+            z_copy(k, 0).wait_recv()
+            for m in relayed:
+                r_copy(k, m).start()
+            s_copy(k, 0, ij).start()
+
     for j in range(pairs_j):
         half[2 * width:, j * width:(j + 1) * width] = u[j].T
 
@@ -206,6 +216,11 @@
     for index in range(n - 1, len(partners)):
         await_ready(index)
     p_copy(0).start()
+    if n > 1:
+        @pl.when(iz == 0)
+        def _():
+            pass_on(1)
+
     @pl.when(iz >= 0)
     def _():
         if n > 1:
@@ -214,23 +229,12 @@
     with jax.named_scope("up"):
         send_up(True, False, iz == 0)
 
-    def pass_on(i):
-        k = order[i]
-        with jax.named_scope("pass%d" % i):
-            z_copy(k, 0).wait_recv()
-            for m in relayed:
-                r_copy(k, m).start()
-            s_copy(k, 0, ij).start()
-
     def share(i):
         k = order[i]
-        with jax.named_scope("shareA%d" % i):
-            for m in direct[1:]:
-                z_copy(k, m).wait_recv()
-                s_copy(k, m, ij).start()
-        with jax.named_scope("shareB%d" % i):
-            for m in relayed:
-                r_copy(k, m, m).wait_recv()
+        with jax.named_scope("share%d" % i):
+            if len(spots) > 1:
+                sent(k, len(spots) - 1, late_recv).wait()
+            for m in direct[1:] + relayed:
                 s_copy(k, m, ij).start()
 
     def complete(i):
@@ -257,8 +261,11 @@
             lat[lat_half(core), :] = mine.astype(BF16)
 
     chip_latent()
-    for i in range(1, min(2, n)):
-        pass_on(i)
+    if n > 1:
+        @pl.when(iz > 0)
+        def _():
+            pass_on(1)
+
     send_up(False, False, iz >= 0)
     for i in range(2, min(4, n)):
         pass_on(i)
@@ -271,7 +278,11 @@
         @pl.when(iz >= 0)
         def _():
             halfway(order[i], 0, early)
-        share(i + 1)
+
+        @pl.when(iz == 0)
+        def _():
+            share(i + 1)
+
         @pl.when(iz >= 0)
         def _():
             halfway(order[i], 0, late)
@@ -280,6 +291,11 @@
         @pl.when(iz >= 0)
         def _():
             ladder(order[i], early, True)
+
+        @pl.when(iz > 0)
+        def _():
+            share(i + 1)
+
         if i == last[0] - 1 and len(last) > 1:
             share(last[1])
         @pl.when(iz >= 0)
@@ -302,10 +318,7 @@
 
     with jax.named_scope("tail"):
         for k in range(1, n):
-            sent(k, len(direct), z_send).wait()
-            if relayed:
-                sent(k, len(relayed), r_send).wait()
-            sent(k, len(spots), s_send).wait()
+            sent(k, 2 * len(spots), sends).wait()
         for x in range(1, nx):
             p_copy(x).wait_send()
         l_copy(core).wait_send()
@@ -317,7 +330,6 @@
     nx = nj // CORES
     ny = grps if width % (grps * nj * 16) == 0 else 1
     others = max(n - 1, 1)
-    ahead = 1 + (nx - 1) * (ny - 1)
     dma = pltpu.SemaphoreType.DMA
     flag = pltpu.SemaphoreType.REGULAR
     hbm = pl.BlockSpec(memory_space=pltpu.HBM)
@@ -339,10 +351,8 @@
             pltpu.VMEM((nx, width // CORES, rank), BF16),
             pltpu.VMEM((width, rank), BF16),
             dma((2,)), dma((pairs_j,)),
-            flag((n,)), flag((nx,)), flag((ny,)), flag,
-            dma((others,)), dma((others * ahead,)),
-            dma((others,)), dma((others * max(nx * ny - ahead, 1),)),
-            dma((others,)), dma((others,)),
+            flag((others,)), flag((max(nx - 1, 1),)), flag((max(ny - 1, 1),)), flag,
+            dma((others,)), dma((others,)), dma((others,)), dma((others,)),
             dma((nx,)), dma((nx,)),
             dma, dma,
         ],

time: 17.9 us -> 17.8 us (level)
  the two profiles are of different devices: /device:TPU:27 before, /device:TPU:0 now
where the time goes in v4:
time: 17.8 us; the launch traced here: 17.7 us
  Pallas kernels  16.7 us (94%)
  local copies, waits for them, and re-layouts  1.02 us (6%)
    pallas_call x1, Pallas kernels, shards(): pl.pallas_call(functools.partial(sigma_kernel, n, nj, ny), out_shape=pltp...  16.7 us
    unnamed x1, local copies, waits for them, and re-layouts  1.02 us

profile of v4, /device:TPU:0, one launch (start us, length us, event | category | flops | bytes accessed | tf_op | source)
XLA Modules:
  0.0 17.7 jit_solution(8392469200841053167)
XLA Ops:
  0.0 16.7 %shard_map.37 = bf16[1,4,384,384]{3,2,1,0:T(8,128)(2,1)S(1)} custom-call(bf16[1,4,384,384]{3,2,1,0:T(8,128)(2,1)} %d_hbm.1, bf16[1,384,384]{2,1,0:T(8,128)(2,1)} %aux_hbm.1, bf16[16,384,128]{2,1,0:T(8,128)(2,1)} %u_hbm.1), custom_call_target="tpu_custom_call" | custom-call | flops 3925868544 | bytes 2359296 | tf_op jit(solution)/shard_map/pallas_call | solution.py:337
  16.7 1.0 %copy.5 = bf16[1,4,384,384]{3,2,1,0:T(8,128)(2,1)} copy(bf16[1,4,384,384]{3,2,1,0:T(8,128)(2,1)S(1)} %shard_map.37) | data formatting | bytes 2359296

commit v5 on v4

--- a/solution.py
+++ b/solution.py
@@ -173,6 +173,19 @@
     load_aux.wait()
     send_down(3)
     send_up(True, True, iz > 0)
+    sibling_index = n - 1 + nx - 1
+    await_ready(sibling_index)
+    p_copy(0).start()
+
+    def chip_latent():
+        p_copy(0).wait_recv()
+        lat_own[...] += lat_sib[...].astype(F32)
+        p_copy(0).wait_send()
+        plat[...] = lat_own[...].astype(BF16)
+
+    def cross_latent():
+        for x in range(1, nx):
+            p_copy(x).start()
 
     def halfway(k, place, pairs):
         for j in pairs:
@@ -214,8 +227,9 @@
     send_up(True, True, iz == 0)
     send_up(True, False, iz > 0)
     for index in range(n - 1, len(partners)):
-        await_ready(index)
-    p_copy(0).start()
+        if index != sibling_index:
+            await_ready(index)
+    chip_latent()
     if n > 1:
         @pl.when(iz == 0)
         def _():
@@ -225,6 +239,7 @@
     def _():
         if n > 1:
             ladder(0, every, False)
+    cross_latent()
     send_down(5)
     with jax.named_scope("up"):
         send_up(True, False, iz == 0)
@@ -242,16 +257,6 @@
         with jax.named_scope("compl%d" % i):
             sent(k, len(spots), s_recv).wait()
 
-    def chip_latent():
-        p_copy(0).wait_recv()
-        lat_own[...] += lat_sib[...].astype(F32)
-        p_copy(0).wait_send()
-        plat[...] = lat_own[...].astype(BF16)
-
-    def cross_latent():
-        for x in range(1, nx):
-            p_copy(x).start()
-
     def whole_latent():
         with jax.named_scope("wholelat"):
             mine = lat_own[lat_half(core), :]
@@ -260,7 +265,6 @@
                 mine += lat_in[x].astype(F32)
             lat[lat_half(core), :] = mine.astype(BF16)
 
-    chip_latent()
     if n > 1:
         @pl.when(iz > 0)
         def _():
@@ -269,7 +273,6 @@
     send_up(False, False, iz >= 0)
     for i in range(2, min(4, n)):
         pass_on(i)
-    cross_latent()
     for i in range(1, min(2, n)):
         share(i)
     last = list(range(max(n - 2, min(n - 1, 1)), n))
@@ -279,10 +282,6 @@
         def _():
             halfway(order[i], 0, early)
 
-        @pl.when(iz == 0)
-        def _():
-            share(i + 1)
-
         @pl.when(iz >= 0)
         def _():
             halfway(order[i], 0, late)
@@ -292,10 +291,7 @@
         def _():
             ladder(order[i], early, True)
 
-        @pl.when(iz > 0)
-        def _():
-            share(i + 1)
-
+        share(i + 1)
         if i == last[0] - 1 and len(last) > 1:
             share(last[1])
         @pl.when(iz >= 0)

time: 17.8 us -> 17.7 us (level)
  Pallas kernels: 16.7 us -> 16.4 us
    pallas_call x1, Pallas kernels: 16.7 us -> 16.4 us  [shards(): pl.pallas_call(functools.partial(sigma_kernel, n, nj, ny), out_shape=pltp...]
where the time goes in v5:
time: 17.7 us; the launch traced here: 17.5 us
  Pallas kernels  16.4 us (93%)
  local copies, waits for them, and re-layouts  1.02 us (6%)
    pallas_call x1, Pallas kernels, shards(): pl.pallas_call(functools.partial(sigma_kernel, n, nj, ny), out_shape=pltp...  16.4 us
    unnamed x1, local copies, waits for them, and re-layouts  1.02 us

profile of v5, /device:TPU:0, one launch (start us, length us, event | category | flops | bytes accessed | tf_op | source)
XLA Modules:
  0.0 17.5 jit_solution(10418354501491618651)
XLA Ops:
  0.0 16.4 %shard_map.37 = bf16[1,4,384,384]{3,2,1,0:T(8,128)(2,1)S(1)} custom-call(bf16[1,4,384,384]{3,2,1,0:T(8,128)(2,1)} %d_hbm.1, bf16[1,384,384]{2,1,0:T(8,128)(2,1)} %aux_hbm.1, bf16[16,384,128]{2,1,0:T(8,128)(2,1)} %u_hbm.1), custom_call_target="tpu_custom_call" | custom-call | flops 3925868544 | bytes 2359296 | tf_op jit(solution)/shard_map/pallas_call | solution.py:333
  16.4 1.0 %copy.5 = bf16[1,4,384,384]{3,2,1,0:T(8,128)(2,1)} copy(bf16[1,4,384,384]{3,2,1,0:T(8,128)(2,1)S(1)} %shard_map.37) | data formatting | bytes 2359296

commit v6 on v5

--- a/solution.py
+++ b/solution.py
@@ -280,11 +280,8 @@
         complete(i)
         @pl.when(iz >= 0)
         def _():
-            halfway(order[i], 0, early)
-
-        @pl.when(iz >= 0)
-        def _():
-            halfway(order[i], 0, late)
+            halfway(order[i], 0, every)
+
         if i + 3 < n:
             pass_on(i + 3)
         @pl.when(iz >= 0)
@@ -297,6 +294,7 @@
         @pl.when(iz >= 0)
         def _():
             ladder(order[i], late, True)
+
     whole_latent()
     l_copy(core).start()
     if last[0] == 1 and len(last) > 1:

time: 17.7 us -> 17.7 us (level)
  no operation moved by 1% of the time
where the time goes in v6:
time: 17.7 us; the launch traced here: 17.5 us
  Pallas kernels  16.4 us (93%)
  local copies, waits for them, and re-layouts  1.02 us (6%)
    pallas_call x1, Pallas kernels, shards(): pl.pallas_call(functools.partial(sigma_kernel, n, nj, ny), out_shape=pltp...  16.4 us
    unnamed x1, local copies, waits for them, and re-layouts  1.02 us

profile of v6, /device:TPU:0, one launch (start us, length us, event | category | flops | bytes accessed | tf_op | source)
XLA Modules:
  0.0 17.5 jit_solution(10418354501491618651)
XLA Ops:
  0.0 16.4 %shard_map.37 = bf16[1,4,384,384]{3,2,1,0:T(8,128)(2,1)S(1)} custom-call(bf16[1,4,384,384]{3,2,1,0:T(8,128)(2,1)} %d_hbm.1, bf16[1,384,384]{2,1,0:T(8,128)(2,1)} %aux_hbm.1, bf16[16,384,128]{2,1,0:T(8,128)(2,1)} %u_hbm.1), custom_call_target="tpu_custom_call" | custom-call | flops 3925868544 | bytes 2359296 | tf_op jit(solution)/shard_map/pallas_call | solution.py:331
  16.4 1.0 %copy.5 = bf16[1,4,384,384]{3,2,1,0:T(8,128)(2,1)} copy(bf16[1,4,384,384]{3,2,1,0:T(8,128)(2,1)S(1)} %shard_map.37) | data formatting | bytes 2359296
